TPU v7x, 32 devices: a whole 2x2x4 slice. The times are simulated.
32 devices in a mesh: wide: 16 (over z, x, core), lev: 2 (over y).
Axes of the slice: x: 2, y: 2, z: 4, core: 2. Of those that a mesh axis runs over, the one named last changes fastest.
Arguments:
- member_control: float32 [16, 16, 128], P('wide'), may hold values from -6 to 6
- static_control: float32 [8, 128, 1024], P('lev', 'wide'), may hold values from -6 to 6
- perturbations: bfloat16 [16, 8, 128, 1024], P(None, 'lev', 'wide'), may hold values from -6 to 6
- innovation: float32 [8, 128, 1024], P('lev', 'wide'), may hold values from -9 to 9
- diffusivity: float32 [8, 128, 1024], P('lev', 'wide'), may hold values from 0.05 to 0.15
- rows_factor: float32 [16, 16], replicated, may hold values from -1.5 to 1.5
- column_factor: float32 [128, 128], replicated, may hold values from -0.5 to 0.5
- ocean_mask: int32 [128, 1024], P('wide'), may hold values 0 or 1
- huber_blocks: int32 [8, 16, 128], P('lev', 'wide'), may hold values 0 or 1
- fold_map: int32 [1024], replicated, may hold values from 0 to 1023, as said below
Outputs:
- increment: float32 [8, 128, 1024], P('lev', 'wide')
- member_gradient: float32 [16, 16, 128], P('wide')
- static_gradient: float32 [8, 128, 1024], P('lev', 'wide')
Inputs may be any that keep to these rules, and one draw needn't show every extreme that they name: fold_map[fold_map[j]] = j and fold_map[j] != j for every column j.
All inputs are finite; a program needn't handle non-finite values. No bound on the sum of `ocean_mask` or of `huber_blocks` on one device may be relied on, other than what follows from the above.
Results may differ from a plain program's by a relative error of at most 0.0003.
Values sent between devices are 32-bit elements; how exact they have to be, the bound alone decides.
No kernel may reach another device: no remote copies, remote signals or barrier semaphores. Data moves between devices by JAX's collectives and lax.ppermute only.
A program may use at most 64 MiB of HBM per device.

v0:
```python
import jax
import jax.numpy as jnp
from jax import lax
from jax.sharding import PartitionSpec as P

REFINE = 8
STEPS = 3
HUBER_EDGE = 1.0
VERTICAL_WEIGHT = 0.5
PRECISE = lax.Precision.HIGHEST


def with_halo(array, sides, width):
    for axis, dim in sides:
        count, length = (lax.axis_size(axis), array.shape[dim])
        up = [(i, (i + 1) % count) for i in range(count - 1)]
        down = [(j, i) for i, j in up]
        last = lax.slice_in_dim(array, length - width, length, axis=dim)
        first = lax.slice_in_dim(array, 0, width, axis=dim)
        before = lax.ppermute(last, axis, up)
        after = lax.ppermute(first, axis, down)
        array = jnp.concatenate([before, array, after], axis=dim)
    return array


def smooth_fields(values, rows_factor, column_factor):
    left_done = jnp.einsum("ij,mjk->mik", rows_factor, values, precision=PRECISE)
    return jnp.einsum("mik,kl->mil", left_done, column_factor, precision=PRECISE)


def smooth_adjoint(values, rows_factor, column_factor):
    left_done = jnp.einsum("ji,mjk->mik", rows_factor, values, precision=PRECISE)
    return jnp.einsum("mik,lk->mil", left_done, column_factor, precision=PRECISE)


def interpolate(extended, refine):
    fraction = jnp.arange(refine, dtype=jnp.float32) / refine
    below_row = extended[..., :-1, None, :]
    above_row = extended[..., 1:, None, :]
    row_terms = below_row * (1.0 - fraction)[:, None] + above_row * fraction[:, None]
    dims_of = row_terms.shape
    row_terms = row_terms.reshape(dims_of[:-3] + (dims_of[-3] * refine, dims_of[-1]))
    wrapped = jnp.roll(row_terms, -1, axis=-1)
    col_terms = row_terms[..., None] * (1.0 - fraction) + wrapped[..., None] * fraction
    return col_terms.reshape(row_terms.shape[:-1] + (row_terms.shape[-1] * refine,))


def interpolate_adjoint(fine_field, refine):
    fraction = jnp.arange(refine, dtype=jnp.float32) / refine
    dims_of = fine_field.shape
    col_terms = fine_field.reshape(dims_of[:-1] + (dims_of[-1] // refine, refine))
    coarse_cols = jnp.sum(col_terms * (1.0 - fraction), axis=-1) + jnp.roll(
        jnp.sum(col_terms * fraction, axis=-1), 1, axis=-1
    )
    row_terms = coarse_cols.reshape(
        dims_of[:-2] + (dims_of[-2] // refine, refine, dims_of[-1] // refine)
    )
    below_part = jnp.sum(row_terms * (1.0 - fraction)[:, None], axis=-2)
    above_part = jnp.sum(row_terms * fraction[:, None], axis=-2)
    zero_row = jnp.zeros_like(below_part)
    return jnp.concatenate([below_part, zero_row], axis=-2) + jnp.concatenate(
        [zero_row, above_part], axis=-2
    )


def diffuse(values, diffusivity, fold_map):
    is_last = lax.axis_index("wide") == lax.axis_size("wide") - 1
    root_kappa = jnp.sqrt(diffusivity)
    for _ in range(STEPS):
        scaled = root_kappa * values
        padded = with_halo(scaled, (("wide", 1), ("lev", 0)), 1)
        folded = jnp.take(scaled[:, -1, :], fold_map, axis=1)
        padded = padded.at[1:-1, -1, :].set(jnp.where(is_last, folded, padded[1:-1, -1, :]))
        across = (
            padded[1:-1, 2:, :]
            + padded[1:-1, :-2, :]
            + jnp.roll(scaled, 1, axis=2)
            + jnp.roll(scaled, -1, axis=2)
            - 4.0 * scaled
        )
        vertical = padded[2:, 1:-1, :] + padded[:-2, 1:-1, :] - 2.0 * scaled
        values = values + root_kappa * (across + VERTICAL_WEIGHT * vertical)
    return values


def huber_weigh(increment, innovation, ocean_cells, huber_blocks):
    misfit = increment - innovation
    expanded = jnp.repeat(jnp.repeat(huber_blocks, REFINE, axis=1), REFINE, axis=2)
    weight = jnp.where(expanded == 1, HUBER_EDGE / jnp.maximum(jnp.abs(misfit), HUBER_EDGE), 1.0)
    return ocean_cells * weight * misfit


def on_device(
    member_control,
    static_control,
    perturbations,
    innovation,
    diffusivity,
    rows_factor,
    column_factor,
    ocean_mask,
    huber_blocks,
    fold_map,
):
    members = perturbations.shape[0]
    member_scale = (members - 1) ** (-0.5)
    wide_count = lax.axis_size("wide")
    smoothed = smooth_fields(member_control, rows_factor, column_factor)
    held, coarse_rows, width = smoothed.shape
    tile_rows = coarse_rows // wide_count
    main_rows = smoothed.reshape(held, wide_count, tile_rows, width)
    next_rows = jnp.concatenate([smoothed[:, tile_rows::tile_rows, :], smoothed[:, -1:, :]], axis=1)
    windows = jnp.concatenate([main_rows, next_rows[:, :, None, :]], axis=2)
    arrived = lax.all_to_all(windows, "wide", split_axis=1, concat_axis=0, tiled=True)
    extended = arrived.reshape(members, tile_rows + 1, width)
    fine_field = interpolate(extended, REFINE)
    ensemble = jnp.sum(fine_field[:, None] * perturbations, axis=0)
    ocean_cells = ocean_mask.astype(jnp.float32)
    increment = ocean_cells * (
        member_scale * ensemble + diffuse(static_control, diffusivity, fold_map)
    )
    weighted = huber_weigh(increment, innovation, ocean_cells, huber_blocks)
    static_gradient = static_control + diffuse(weighted, diffusivity, fold_map)
    fine_terms = jnp.sum(perturbations * weighted[None], axis=1) * member_scale
    level_part = interpolate_adjoint(fine_terms, REFINE)
    ext_grad = lax.psum(level_part, "lev")
    windows = lax.all_to_all(ext_grad[:, None], "wide", split_axis=0, concat_axis=1, tiled=True)
    main_rows = windows[:, :, :tile_rows, :]
    next_rows = windows[:, :, tile_rows, :]
    main_rows = main_rows.at[:, 1:, 0, :].add(next_rows[:, :-1, :])
    main_rows = main_rows.at[:, -1, tile_rows - 1, :].add(next_rows[:, -1, :])
    smooth_grad = main_rows.reshape(held, coarse_rows, width)
    member_gradient = member_control + smooth_adjoint(smooth_grad, rows_factor, column_factor)
    return (increment, member_gradient, static_gradient)


def solution(mesh):
    return jax.shard_map(
        on_device,
        mesh=mesh,
        in_specs=(
            P("wide", None, None),
            P("lev", "wide", None),
            P(None, "lev", "wide", None),
            P("lev", "wide", None),
            P("lev", "wide", None),
            P(),
            P(),
            P("wide", None),
            P("lev", "wide", None),
            P(),
        ),
        out_specs=(P("lev", "wide", None), P("wide", None, None), P("lev", "wide", None)),
        check_vma=False,
    )
```

profile of v0, /device:TPU:0, one launch (start us, length us, event | category | flops | bytes accessed | tf_op | source)
XLA Modules:
  0.0 148.4 jit_solution(14129248455665932806)
XLA Ops:
  4.0 3.0 %collective-permute-start = (f32[4,1,1024]{2,0,1:T(4,128)S(1)}, f32[4,1,1024]{2,0,1:T(4,128)S(1)}, u32[]{:S(2)}, u32[]{:S(2)}) collective-permute-start(f32[4,1,1024]{2,0,1:T(4,128)S(1)} %get-tuple-element.178), channel_id=1, source_target_pairs={{0,2},{2,4},{4,6},{6,8},{8,10},{10,12},{12,14},{14,16},{16,18},{18... | collective-permute-start | bytes 49160 | tf_op jit(solution)/shard_map/ppermute | solution.py:20
  8.7 8.0 %all-to-all-start = ((f32[1,16,2,128]{3,2,0,1:T(2,128)}), f32[1,16,2,128]{3,2,0,1:T(2,128)S(1)}, u32[]{:S(2)}, u32[]{:S(2)}) async-start(f32[1,16,2,128]{3,2,0,1:T(2,128)} %copy.546), calls=%async_computation | async-start | bytes 32768 | tf_op jit(solution)/shard_map/all_to_all | solution.py:114
  19.2 2.8 %gather_fusion = f32[1024,4]{1,0:T(8,128)S(1)} fusion(f32[4,1024]{0,1:T(8,128)S(1)} %copy.555, s32[1024]{0:T(1024)S(1)} %fusion.62), kind=kCustom, calls=%fused_computation.clone | custom fusion | bytes 36864 | tf_op jit(solution)/shard_map/jit(_take)/gather | solution.py:72
  23.6 3.4 %collective-permute-start.2 = (f32[1,10,1024]{2,0,1:T(1,128)S(1)}, f32[1,10,1024]{2,0,1:T(1,128)S(1)}, u32[]{:S(2)}, u32[]{:S(2)}) collective-permute-start(f32[1,10,1024]{2,0,1:T(1,128)S(1)} %get-tuple-element.135), channel_id=1, source_target_pairs={{0,1},{2,3},{4,5},{6,7},{8,9},{10,11},{12,13},{14,15},{16,17},{18,... | collective-permute-start | bytes 122888 | tf_op jit(solution)/shard_map/ppermute | solution.py:20
  31.9 2.9 %copy.552 = f32[16,8,1024]{2,1,0:T(8,128)S(1)} copy(f32[16,8,1024]{0,2,1:T(8,128)} %fusion.2) | data formatting | bytes 1048576 | tf_op jit(solution)/shard_map/add | solution.py:44
  37.2 3.0 %collective-permute-start.4 = (f32[4,1,1024]{2,0,1:T(4,128)S(1)}, f32[4,1,1024]{2,0,1:T(4,128)S(1)}, u32[]{:S(2)}, u32[]{:S(2)}) collective-permute-start(f32[4,1,1024]{2,0,1:T(4,128)S(1)} %get-tuple-element.171), channel_id=1, source_target_pairs={{0,2},{2,4},{4,6},{6,8},{8,10},{10,12},{12,14},{14,16},{16,18},{18... | collective-permute-start | bytes 49160 | tf_op jit(solution)/shard_map/ppermute | solution.py:20
  40.5 2.8 %gather_fusion.1 = f32[1024,4]{1,0:T(8,128)S(1)} fusion(f32[4,1024]{0,1:T(8,128)S(1)} %copy.563, s32[1024]{0:T(1024)S(1)} %fusion.62), kind=kCustom, calls=%fused_computation.1.clone | custom fusion | bytes 36864 | tf_op jit(solution)/shard_map/jit(_take)/gather | solution.py:72
  43.6 4.5 %collective-permute-start.6 = (f32[1,10,1024]{2,0,1:T(1,128)S(1)}, f32[1,10,1024]{2,0,1:T(1,128)S(1)}, u32[]{:S(2)}, u32[]{:S(2)}) collective-permute-start(f32[1,10,1024]{2,0,1:T(1,128)S(1)} %get-tuple-element.133), channel_id=1, source_target_pairs={{0,1},{2,3},{4,5},{6,7},{8,9},{10,11},{12,13},{14,15},{16,17},{18,... | collective-permute-start | bytes 122888 | tf_op jit(solution)/shard_map/ppermute | solution.py:20
  49.8 4.4 %collective-permute-done.7 = f32[1,10,1024]{2,0,1:T(1,128)S(1)} collective-permute-done((f32[1,10,1024]{2,0,1:T(1,128)S(1)}, f32[1,10,1024]{2,0,1:T(1,128)S(1)}, u32[]{:S(2)}, u32[]{:S(2)}) %collective-permute-start.7) | collective-permute-done | bytes 40992 | tf_op jit(solution)/shard_map/ppermute | solution.py:21
  56.3 3.0 %collective-permute-start.8 = (f32[4,1,1024]{2,0,1:T(4,128)S(1)}, f32[4,1,1024]{2,0,1:T(4,128)S(1)}, u32[]{:S(2)}, u32[]{:S(2)}) collective-permute-start(f32[4,1,1024]{2,0,1:T(4,128)S(1)} %get-tuple-element.164), channel_id=1, source_target_pairs={{0,2},{2,4},{4,6},{6,8},{8,10},{10,12},{12,14},{14,16},{16,18},{18... | collective-permute-start | bytes 49160 | tf_op jit(solution)/shard_map/ppermute | solution.py:20
  59.6 2.8 %gather_fusion.2 = f32[1024,4]{1,0:T(8,128)S(1)} fusion(f32[4,1024]{0,1:T(8,128)S(1)} %copy.570, s32[1024]{0:T(1024)S(1)} %fusion.62), kind=kCustom, calls=%fused_computation.2.clone | custom fusion | bytes 36864 | tf_op jit(solution)/shard_map/jit(_take)/gather | solution.py:72
  65.8 4.3 %collective-permute-done.11 = f32[1,10,1024]{2,0,1:T(1,128)S(1)} collective-permute-done((f32[1,10,1024]{2,0,1:T(1,128)S(1)}, f32[1,10,1024]{2,0,1:T(1,128)S(1)}, u32[]{:S(2)}, u32[]{:S(2)}) %collective-permute-start.11) | collective-permute-done | bytes 40992 | tf_op jit(solution)/shard_map/ppermute | solution.py:21
  72.3 2.8 %gather_fusion.3 = f32[1024,4]{1,0:T(8,128)S(1)} fusion(f32[4,1024]{0,1:T(8,128)S(1)} %copy.583, s32[1024]{0:T(1024)S(1)} %fusion.62), kind=kCustom, calls=%fused_computation.3.clone | custom fusion | bytes 36864 | tf_op jit(solution)/shard_map/jit(_take)/gather | solution.py:72
  76.6 3.0 %collective-permute-start.12 = (f32[4,1,1024]{2,0,1:T(4,128)S(1)}, f32[4,1,1024]{2,0,1:T(4,128)S(1)}, u32[]{:S(2)}, u32[]{:S(2)}) collective-permute-start(f32[4,1,1024]{2,0,1:T(4,128)S(1)} %get-tuple-element.157), channel_id=1, source_target_pairs={{0,2},{2,4},{4,6},{6,8},{8,10},{10,12},{12,14},{14,16},{16,18},{18... | collective-permute-start | bytes 49160 | tf_op jit(solution)/shard_map/ppermute | solution.py:20
  82.3 5.0 %fusion.1 = (f32[16,8,128]{0,2,1:T(8,128)S(1)}, f32[16,8,128]{0,2,1:T(8,128)S(1)}) fusion(f32[16,8,1024]{0,2,1:T(8,128)} %copy.577, f32[8]{0:T(128)S(1)} %get-tuple-element.185, f32[8]{0:T(128)S(1)} %get-tuple-element.186), kind=kLoop, calls=%fused_computation.9 | loop fusion | flops 491520 | bytes 655424 | tf_op jit(solution)/shard_map/reduce_sum | solution.py:53
  87.6 8.9 %psum.7 = f32[16,1,2,128]{0,3,2,1:T(8,128)S(1)} all-reduce(f32[16,1,2,128]{0,3,2,1:T(8,128)S(1)} %add_bitcast_fusion), channel_id=1, replica_groups=mesh['wide'=16,'lev'=2] {'lev'}, use_global_device_ids=true, to_apply=%region_6.8 | all-reduce | flops 4096 | bytes 32768 | tf_op jit(solution)/shard_map/psum | solution.py:126
  97.2 6.2 %all-to-all-start.1 = ((f32[16,1,2,128]{3,2,1,0:T(2,128)}), f32[16,1,2,128]{3,2,1,0:T(2,128)S(1)}, u32[]{:S(2)}, u32[]{:S(2)}) async-start(f32[16,1,2,128]{3,2,1,0:T(2,128)} %copy.578), calls=%async_computation.1 | async-start | bytes 32768 | tf_op jit(solution)/shard_map/all_to_all | solution.py:127
  103.6 3.9 %collective-permute-start.14 = (f32[1,10,1024]{2,0,1:T(1,128)S(1)}, f32[1,10,1024]{2,0,1:T(1,128)S(1)}, u32[]{:S(2)}, u32[]{:S(2)}) collective-permute-start(f32[1,10,1024]{2,0,1:T(1,128)S(1)} %get-tuple-element.129), channel_id=1, source_target_pairs={{0,1},{2,3},{4,5},{6,7},{8,9},{10,11},{12,13},{14,15},{16,17},{18,... | collective-permute-start | bytes 122888 | tf_op jit(solution)/shard_map/ppermute | solution.py:20
  115.7 3.0 %collective-permute-start.16 = (f32[4,1,1024]{2,0,1:T(4,128)S(1)}, f32[4,1,1024]{2,0,1:T(4,128)S(1)}, u32[]{:S(2)}, u32[]{:S(2)}) collective-permute-start(f32[4,1,1024]{2,0,1:T(4,128)S(1)} %get-tuple-element.150), channel_id=1, source_target_pairs={{0,2},{2,4},{4,6},{6,8},{8,10},{10,12},{12,14},{14,16},{16,18},{18... | collective-permute-start | bytes 49160 | tf_op jit(solution)/shard_map/ppermute | solution.py:20
  119.1 2.8 %gather_fusion.4 = f32[1024,4]{1,0:T(8,128)S(1)} fusion(f32[4,1024]{0,1:T(8,128)S(1)} %copy.592, s32[1024]{0:T(1024)S(1)} %fusion.62), kind=kCustom, calls=%fused_computation.4.clone | custom fusion | bytes 36864 | tf_op jit(solution)/shard_map/jit(_take)/gather | solution.py:72
  126.1 4.5 %collective-permute-done.19 = f32[1,10,1024]{2,0,1:T(1,128)S(1)} collective-permute-done((f32[1,10,1024]{2,0,1:T(1,128)S(1)}, f32[1,10,1024]{2,0,1:T(1,128)S(1)}, u32[]{:S(2)}, u32[]{:S(2)}) %collective-permute-start.19) | collective-permute-done | bytes 40992 | tf_op jit(solution)/shard_map/ppermute | solution.py:21
  132.8 3.0 %collective-permute-start.20 = (f32[4,1,1024]{2,0,1:T(4,128)S(1)}, f32[4,1,1024]{2,0,1:T(4,128)S(1)}, u32[]{:S(2)}, u32[]{:S(2)}) collective-permute-start(f32[4,1,1024]{2,0,1:T(4,128)S(1)} %get-tuple-element.143), channel_id=1, source_target_pairs={{0,2},{2,4},{4,6},{6,8},{8,10},{10,12},{12,14},{14,16},{16,18},{18... | collective-permute-start | bytes 49160 | tf_op jit(solution)/shard_map/ppermute | solution.py:20
  136.2 2.8 %gather_fusion.5 = f32[1024,4]{1,0:T(8,128)S(1)} fusion(f32[4,1024]{0,1:T(8,128)S(1)} %copy.603, s32[1024]{0:T(1024)S(1)} %fusion.62), kind=kCustom, calls=%fused_computation.5.clone | custom fusion | bytes 36864 | tf_op jit(solution)/shard_map/jit(_take)/gather | solution.py:72
  142.6 4.5 %collective-permute-done.23 = f32[1,10,1024]{2,0,1:T(1,128)S(1)} collective-permute-done((f32[1,10,1024]{2,0,1:T(1,128)S(1)}, f32[1,10,1024]{2,0,1:T(1,128)S(1)}, u32[]{:S(2)}, u32[]{:S(2)}) %collective-permute-start.23) | collective-permute-done | bytes 40992 | tf_op jit(solution)/shard_map/ppermute | solution.py:21
  (178 shorter events, 51.0 us)
Async XLA Ops:
  2.7 20.8 %collective-permute-start.1 = (f32[4,1,1024]{2,0,1:T(4,128)S(1)}, f32[4,1,1024]{2,0,1:T(4,128)S(1)}, u32[]{:S(2)}, u32[]{:S(2)}) collective-permute-start(f32[4,1,1024]{2,0,1:T(4,128)S(1)} %get-tuple-element.177), channel_id=1, source_target_pairs={{2,0},{4,2},{6,4},{8,6},{10,8},{12,10},{14,12},{16,14},{18,16},{20... | collective-permute-start | bytes 49160 | tf_op jit(solution)/shard_map/ppermute | solution.py:21
  4.0 19.5 %collective-permute-start = (f32[4,1,1024]{2,0,1:T(4,128)S(1)}, f32[4,1,1024]{2,0,1:T(4,128)S(1)}, u32[]{:S(2)}, u32[]{:S(2)}) collective-permute-start(f32[4,1,1024]{2,0,1:T(4,128)S(1)} %get-tuple-element.178), channel_id=1, source_target_pairs={{0,2},{2,4},{4,6},{6,8},{8,10},{10,12},{12,14},{14,16},{16,18},{18... | collective-permute-start | bytes 49160 | tf_op jit(solution)/shard_map/ppermute | solution.py:20
  8.7 19.7 %all-to-all-start = ((f32[1,16,2,128]{3,2,0,1:T(2,128)}), f32[1,16,2,128]{3,2,0,1:T(2,128)S(1)}, u32[]{:S(2)}, u32[]{:S(2)}) async-start(f32[1,16,2,128]{3,2,0,1:T(2,128)} %copy.546), calls=%async_computation | async-start | bytes 32768 | tf_op jit(solution)/shard_map/all_to_all | solution.py:114
  23.6 11.4 %collective-permute-start.2 = (f32[1,10,1024]{2,0,1:T(1,128)S(1)}, f32[1,10,1024]{2,0,1:T(1,128)S(1)}, u32[]{:S(2)}, u32[]{:S(2)}) collective-permute-start(f32[1,10,1024]{2,0,1:T(1,128)S(1)} %get-tuple-element.135), channel_id=1, source_target_pairs={{0,1},{2,3},{4,5},{6,7},{8,9},{10,11},{12,13},{14,15},{16,17},{18,... | collective-permute-start | bytes 122888 | tf_op jit(solution)/shard_map/ppermute | solution.py:20
  27.1 8.0 %collective-permute-start.3 = (f32[1,10,1024]{2,0,1:T(1,128)S(1)}, f32[1,10,1024]{2,0,1:T(1,128)S(1)}, u32[]{:S(2)}, u32[]{:S(2)}) collective-permute-start(f32[1,10,1024]{2,0,1:T(1,128)S(1)} %get-tuple-element.136), channel_id=1, source_target_pairs={{1,0},{3,2},{5,4},{7,6},{9,8},{11,10},{13,12},{15,14},{17,16},{19,... | collective-permute-start | bytes 122888 | tf_op jit(solution)/shard_map/ppermute | solution.py:21
  35.9 7.7 %collective-permute-start.5 = (f32[4,1,1024]{2,0,1:T(4,128)S(1)}, f32[4,1,1024]{2,0,1:T(4,128)S(1)}, u32[]{:S(2)}, u32[]{:S(2)}) collective-permute-start(f32[4,1,1024]{2,0,1:T(4,128)S(1)} %get-tuple-element.170), channel_id=1, source_target_pairs={{2,0},{4,2},{6,4},{8,6},{10,8},{12,10},{14,12},{16,14},{18,16},{20... | collective-permute-start | bytes 49160 | tf_op jit(solution)/shard_map/ppermute | solution.py:21
  37.2 6.4 %collective-permute-start.4 = (f32[4,1,1024]{2,0,1:T(4,128)S(1)}, f32[4,1,1024]{2,0,1:T(4,128)S(1)}, u32[]{:S(2)}, u32[]{:S(2)}) collective-permute-start(f32[4,1,1024]{2,0,1:T(4,128)S(1)} %get-tuple-element.171), channel_id=1, source_target_pairs={{0,2},{2,4},{4,6},{6,8},{8,10},{10,12},{12,14},{14,16},{16,18},{18... | collective-permute-start | bytes 49160 | tf_op jit(solution)/shard_map/ppermute | solution.py:20
  43.6 6.2 %collective-permute-start.6 = (f32[1,10,1024]{2,0,1:T(1,128)S(1)}, f32[1,10,1024]{2,0,1:T(1,128)S(1)}, u32[]{:S(2)}, u32[]{:S(2)}) collective-permute-start(f32[1,10,1024]{2,0,1:T(1,128)S(1)} %get-tuple-element.133), channel_id=1, source_target_pairs={{0,1},{2,3},{4,5},{6,7},{8,9},{10,11},{12,13},{14,15},{16,17},{18,... | collective-permute-start | bytes 122888 | tf_op jit(solution)/shard_map/ppermute | solution.py:20
  48.2 6.0 %collective-permute-start.7 = (f32[1,10,1024]{2,0,1:T(1,128)S(1)}, f32[1,10,1024]{2,0,1:T(1,128)S(1)}, u32[]{:S(2)}, u32[]{:S(2)}) collective-permute-start(f32[1,10,1024]{2,0,1:T(1,128)S(1)} %get-tuple-element.134), channel_id=1, source_target_pairs={{1,0},{3,2},{5,4},{7,6},{9,8},{11,10},{13,12},{15,14},{17,16},{19,... | collective-permute-start | bytes 122888 | tf_op jit(solution)/shard_map/ppermute | solution.py:21
  55.0 7.7 %collective-permute-start.9 = (f32[4,1,1024]{2,0,1:T(4,128)S(1)}, f32[4,1,1024]{2,0,1:T(4,128)S(1)}, u32[]{:S(2)}, u32[]{:S(2)}) collective-permute-start(f32[4,1,1024]{2,0,1:T(4,128)S(1)} %get-tuple-element.163), channel_id=1, source_target_pairs={{2,0},{4,2},{6,4},{8,6},{10,8},{12,10},{14,12},{16,14},{18,16},{20... | collective-permute-start | bytes 49160 | tf_op jit(solution)/shard_map/ppermute | solution.py:21
  56.3 6.4 %collective-permute-start.8 = (f32[4,1,1024]{2,0,1:T(4,128)S(1)}, f32[4,1,1024]{2,0,1:T(4,128)S(1)}, u32[]{:S(2)}, u32[]{:S(2)}) collective-permute-start(f32[4,1,1024]{2,0,1:T(4,128)S(1)} %get-tuple-element.164), channel_id=1, source_target_pairs={{0,2},{2,4},{4,6},{6,8},{8,10},{10,12},{12,14},{14,16},{16,18},{18... | collective-permute-start | bytes 49160 | tf_op jit(solution)/shard_map/ppermute | solution.py:20
  64.2 5.9 %collective-permute-start.11 = (f32[1,10,1024]{2,0,1:T(1,128)S(1)}, f32[1,10,1024]{2,0,1:T(1,128)S(1)}, u32[]{:S(2)}, u32[]{:S(2)}) collective-permute-start(f32[1,10,1024]{2,0,1:T(1,128)S(1)} %get-tuple-element.132), channel_id=1, source_target_pairs={{1,0},{3,2},{5,4},{7,6},{9,8},{11,10},{13,12},{15,14},{17,16},{19,... | collective-permute-start | bytes 122888 | tf_op jit(solution)/shard_map/ppermute | solution.py:21
  75.3 28.1 %collective-permute-start.13 = (f32[4,1,1024]{2,0,1:T(4,128)S(1)}, f32[4,1,1024]{2,0,1:T(4,128)S(1)}, u32[]{:S(2)}, u32[]{:S(2)}) collective-permute-start(f32[4,1,1024]{2,0,1:T(4,128)S(1)} %get-tuple-element.156), channel_id=1, source_target_pairs={{2,0},{4,2},{6,4},{8,6},{10,8},{12,10},{14,12},{16,14},{18,16},{20... | collective-permute-start | bytes 49160 | tf_op jit(solution)/shard_map/ppermute | solution.py:21
  76.6 26.8 %collective-permute-start.12 = (f32[4,1,1024]{2,0,1:T(4,128)S(1)}, f32[4,1,1024]{2,0,1:T(4,128)S(1)}, u32[]{:S(2)}, u32[]{:S(2)}) collective-permute-start(f32[4,1,1024]{2,0,1:T(4,128)S(1)} %get-tuple-element.157), channel_id=1, source_target_pairs={{0,2},{2,4},{4,6},{6,8},{8,10},{10,12},{12,14},{14,16},{16,18},{18... | collective-permute-start | bytes 49160 | tf_op jit(solution)/shard_map/ppermute | solution.py:20
  97.2 12.7 %all-to-all-start.1 = ((f32[16,1,2,128]{3,2,1,0:T(2,128)}), f32[16,1,2,128]{3,2,1,0:T(2,128)S(1)}, u32[]{:S(2)}, u32[]{:S(2)}) async-start(f32[16,1,2,128]{3,2,1,0:T(2,128)} %copy.578), calls=%async_computation.1 | async-start | bytes 32768 | tf_op jit(solution)/shard_map/all_to_all | solution.py:127
  103.6 7.9 %collective-permute-start.14 = (f32[1,10,1024]{2,0,1:T(1,128)S(1)}, f32[1,10,1024]{2,0,1:T(1,128)S(1)}, u32[]{:S(2)}, u32[]{:S(2)}) collective-permute-start(f32[1,10,1024]{2,0,1:T(1,128)S(1)} %get-tuple-element.129), channel_id=1, source_target_pairs={{0,1},{2,3},{4,5},{6,7},{8,9},{10,11},{12,13},{14,15},{16,17},{18,... | collective-permute-start | bytes 122888 | tf_op jit(solution)/shard_map/ppermute | solution.py:20
  107.5 5.9 %collective-permute-start.15 = (f32[1,10,1024]{2,0,1:T(1,128)S(1)}, f32[1,10,1024]{2,0,1:T(1,128)S(1)}, u32[]{:S(2)}, u32[]{:S(2)}) collective-permute-start(f32[1,10,1024]{2,0,1:T(1,128)S(1)} %get-tuple-element.130), channel_id=1, source_target_pairs={{1,0},{3,2},{5,4},{7,6},{9,8},{11,10},{13,12},{15,14},{17,16},{19,... | collective-permute-start | bytes 122888 | tf_op jit(solution)/shard_map/ppermute | solution.py:21
  114.4 7.9 %collective-permute-start.17 = (f32[4,1,1024]{2,0,1:T(4,128)S(1)}, f32[4,1,1024]{2,0,1:T(4,128)S(1)}, u32[]{:S(2)}, u32[]{:S(2)}) collective-permute-start(f32[4,1,1024]{2,0,1:T(4,128)S(1)} %get-tuple-element.149), channel_id=1, source_target_pairs={{2,0},{4,2},{6,4},{8,6},{10,8},{12,10},{14,12},{16,14},{18,16},{20... | collective-permute-start | bytes 49160 | tf_op jit(solution)/shard_map/ppermute | solution.py:21
  115.7 6.6 %collective-permute-start.16 = (f32[4,1,1024]{2,0,1:T(4,128)S(1)}, f32[4,1,1024]{2,0,1:T(4,128)S(1)}, u32[]{:S(2)}, u32[]{:S(2)}) collective-permute-start(f32[4,1,1024]{2,0,1:T(4,128)S(1)} %get-tuple-element.150), channel_id=1, source_target_pairs={{0,2},{2,4},{4,6},{6,8},{8,10},{10,12},{12,14},{14,16},{16,18},{18... | collective-permute-start | bytes 49160 | tf_op jit(solution)/shard_map/ppermute | solution.py:20
  122.4 3.7 %collective-permute-start.18 = (f32[1,10,1024]{2,0,1:T(1,128)S(1)}, f32[1,10,1024]{2,0,1:T(1,128)S(1)}, u32[]{:S(2)}, u32[]{:S(2)}) collective-permute-start(f32[1,10,1024]{2,0,1:T(1,128)S(1)} %get-tuple-element.127), channel_id=1, source_target_pairs={{0,1},{2,3},{4,5},{6,7},{8,9},{10,11},{12,13},{14,15},{16,17},{18,... | collective-permute-start | bytes 122888 | tf_op jit(solution)/shard_map/ppermute | solution.py:20
  124.4 6.3 %collective-permute-start.19 = (f32[1,10,1024]{2,0,1:T(1,128)S(1)}, f32[1,10,1024]{2,0,1:T(1,128)S(1)}, u32[]{:S(2)}, u32[]{:S(2)}) collective-permute-start(f32[1,10,1024]{2,0,1:T(1,128)S(1)} %get-tuple-element.128), channel_id=1, source_target_pairs={{1,0},{3,2},{5,4},{7,6},{9,8},{11,10},{13,12},{15,14},{17,16},{19,... | collective-permute-start | bytes 122888 | tf_op jit(solution)/shard_map/ppermute | solution.py:21
  131.5 7.9 %collective-permute-start.21 = (f32[4,1,1024]{2,0,1:T(4,128)S(1)}, f32[4,1,1024]{2,0,1:T(4,128)S(1)}, u32[]{:S(2)}, u32[]{:S(2)}) collective-permute-start(f32[4,1,1024]{2,0,1:T(4,128)S(1)} %get-tuple-element.142), channel_id=1, source_target_pairs={{2,0},{4,2},{6,4},{8,6},{10,8},{12,10},{14,12},{16,14},{18,16},{20... | collective-permute-start | bytes 49160 | tf_op jit(solution)/shard_map/ppermute | solution.py:21
  132.8 6.6 %collective-permute-start.20 = (f32[4,1,1024]{2,0,1:T(4,128)S(1)}, f32[4,1,1024]{2,0,1:T(4,128)S(1)}, u32[]{:S(2)}, u32[]{:S(2)}) collective-permute-start(f32[4,1,1024]{2,0,1:T(4,128)S(1)} %get-tuple-element.143), channel_id=1, source_target_pairs={{0,2},{2,4},{4,6},{6,8},{8,10},{10,12},{12,14},{14,16},{16,18},{18... | collective-permute-start | bytes 49160 | tf_op jit(solution)/shard_map/ppermute | solution.py:20
  140.9 6.2 %collective-permute-start.23 = (f32[1,10,1024]{2,0,1:T(1,128)S(1)}, f32[1,10,1024]{2,0,1:T(1,128)S(1)}, u32[]{:S(2)}, u32[]{:S(2)}) collective-permute-start(f32[1,10,1024]{2,0,1:T(1,128)S(1)} %get-tuple-element.126), channel_id=1, source_target_pairs={{1,0},{3,2},{5,4},{7,6},{9,8},{11,10},{13,12},{15,14},{17,16},{19,... | collective-permute-start | bytes 122888 | tf_op jit(solution)/shard_map/ppermute | solution.py:21
  (9 other events, 157.2 us)
where the time goes:
time: 149 us; the launch traced here: 148 us
  starting transfers between devices  64.7 us (43%)
  local copies, waits for them, and re-layouts  32 us (21%)
  waiting for transfers between devices  22.2 us (15%)
  other arithmetic  16.8 us (11%)
  blocking collectives  8.93 us (6%)
  matrix products  2.02 us (1%)
  between operations  1.71 us (1%)
    ppermute x12, starting transfers between devices, with_halo(): before = lax.ppermute(last, axis, up)  35 us
    ppermute x12, waiting for transfers between devices, with_halo(): after = lax.ppermute(first, axis, down)  19.7 us
    gather x12, local copies, waits for them, and re-layouts, diffuse(): folded = jnp.take(scaled[:, -1, :], fold_map, axis=1)  18 us
    ppermute x12, starting transfers between devices, with_halo(): after = lax.ppermute(first, axis, down)  15.5 us
    psum x1, blocking collectives, on_device(): ext_grad = lax.psum(level_part, 'lev')  8.93 us
    all_to_all x1, starting transfers between devices, on_device(): lax.all_to_all(windows, 'wide', split_axis=1, concat_axis=0, tiled=True)  7.95 us
    all_to_all x1, starting transfers between devices, on_device(): lax.all_to_all(ext_grad[:, None], 'wide', split_axis=0, concat_axis=1, ti...  6.24 us
    reduce_sum x1, other arithmetic, interpolate_adjoint(): jnp.sum(col_terms * fraction, axis=-1)  5.03 us
  transfers between devices with their start and end apart: 26, of which 10 were waited for; matrix products, arithmetic and copies ran while one was open for 26% of the time, Pallas kernels for 0%

commit v1 on v0

--- a/solution.py
+++ b/solution.py
@@ -123,7 +123,8 @@
     static_gradient = static_control + diffuse(weighted, diffusivity, fold_map)
     fine_terms = jnp.sum(perturbations * weighted[None], axis=1) * member_scale
     level_part = interpolate_adjoint(fine_terms, REFINE)
-    ext_grad = lax.psum(level_part, "lev")
+    terms = lax.all_gather(level_part, "lev", axis=0, tiled=False)
+    ext_grad = terms.sum(axis=0)
     windows = lax.all_to_all(ext_grad[:, None], "wide", split_axis=0, concat_axis=1, tiled=True)
     main_rows = windows[:, :, :tile_rows, :]
     next_rows = windows[:, :, tile_rows, :]

time: 149 us -> 144 us (0.966)
  blocking collectives: 8.93 us -> 4.41 us
    psum x1 -> x0, blocking collectives: 8.93 us -> none  [on_device(): ext_grad = lax.psum(level_part, 'lev')]
    all_gather x0 -> x1, blocking collectives: none -> 4.41 us  [on_device(): terms = lax.all_gather(level_part, 'lev', axis=0, tiled=False)]
    ppermute x12, waiting for transfers between devices: 19.7 us -> 17.9 us  [with_halo(): after = lax.ppermute(first, axis, down)]
    all_to_all x1, waiting for transfers between devices: 1.16 us -> 2.9 us  [on_device(): lax.all_to_all(ext_grad[:, None], 'wide', split_axis=0, concat_axis=1, ti...]
    ppermute x12, starting transfers between devices: 35 us -> 33.2 us  [with_halo(): before = lax.ppermute(last, axis, up)]
  transfers between devices with their start and end apart: 26 -> 26, of which waited for: 10 -> 10; matrix products, arithmetic and copies ran while one was open for 26% -> 29% of each run, Pallas kernels for 0% -> 0%
where the time goes in v1:
time: 144 us; the launch traced here: 143 us
  starting transfers between devices  63.6 us (44%)
  local copies, waits for them, and re-layouts  32 us (22%)
  waiting for transfers between devices  22.2 us (15%)
  other arithmetic  16.9 us (12%)
  blocking collectives  4.41 us (3%)
  matrix products  2.02 us (1%)
  between operations  1.71 us (1%)
    ppermute x12, starting transfers between devices, with_halo(): before = lax.ppermute(last, axis, up)  33.2 us
    gather x12, local copies, waits for them, and re-layouts, diffuse(): folded = jnp.take(scaled[:, -1, :], fold_map, axis=1)  18 us
    ppermute x12, waiting for transfers between devices, with_halo(): after = lax.ppermute(first, axis, down)  17.9 us
    ppermute x12, starting transfers between devices, with_halo(): after = lax.ppermute(first, axis, down)  15.5 us
    all_to_all x1, starting transfers between devices, on_device(): lax.all_to_all(windows, 'wide', split_axis=1, concat_axis=0, tiled=True)  7.95 us
    all_to_all x1, starting transfers between devices, on_device(): lax.all_to_all(ext_grad[:, None], 'wide', split_axis=0, concat_axis=1, ti...  6.93 us
    reduce_sum x1, other arithmetic, interpolate_adjoint(): jnp.sum(col_terms * fraction, axis=-1)  5.03 us
    all_gather x1, blocking collectives, on_device(): terms = lax.all_gather(level_part, 'lev', axis=0, tiled=False)  4.41 us
  transfers between devices with their start and end apart: 26, of which 10 were waited for; matrix products, arithmetic and copies ran while one was open for 29% of the time, Pallas kernels for 0%

profile of v1, /device:TPU:0, one launch (start us, length us, event | category | flops | bytes accessed | tf_op | source)
XLA Modules:
  0.0 142.9 jit_solution(11908295344961641848)
XLA Ops:
  4.0 3.0 %collective-permute-start = (f32[4,1,1024]{2,0,1:T(4,128)S(1)}, f32[4,1,1024]{2,0,1:T(4,128)S(1)}, u32[]{:S(2)}, u32[]{:S(2)}) collective-permute-start(f32[4,1,1024]{2,0,1:T(4,128)S(1)} %get-tuple-element.181), channel_id=1, source_target_pairs={{0,2},{2,4},{4,6},{6,8},{8,10},{10,12},{12,14},{14,16},{16,18},{18... | collective-permute-start | bytes 49160 | tf_op jit(solution)/shard_map/ppermute | solution.py:20
  8.7 8.0 %all-to-all-start = ((f32[1,16,2,128]{3,2,0,1:T(2,128)}), f32[1,16,2,128]{3,2,0,1:T(2,128)S(1)}, u32[]{:S(2)}, u32[]{:S(2)}) async-start(f32[1,16,2,128]{3,2,0,1:T(2,128)} %copy.656), calls=%async_computation | async-start | bytes 32768 | tf_op jit(solution)/shard_map/all_to_all | solution.py:114
  19.2 2.8 %gather_fusion = f32[1024,4]{1,0:T(8,128)S(1)} fusion(f32[4,1024]{0,1:T(8,128)S(1)} %copy.665, s32[1024]{0:T(1024)S(1)} %fusion.62), kind=kCustom, calls=%fused_computation.clone | custom fusion | bytes 36864 | tf_op jit(solution)/shard_map/jit(_take)/gather | solution.py:72
  23.6 3.4 %collective-permute-start.2 = (f32[1,10,1024]{2,0,1:T(1,128)S(1)}, f32[1,10,1024]{2,0,1:T(1,128)S(1)}, u32[]{:S(2)}, u32[]{:S(2)}) collective-permute-start(f32[1,10,1024]{2,0,1:T(1,128)S(1)} %get-tuple-element.138), channel_id=1, source_target_pairs={{0,1},{2,3},{4,5},{6,7},{8,9},{10,11},{12,13},{14,15},{16,17},{18,... | collective-permute-start | bytes 122888 | tf_op jit(solution)/shard_map/ppermute | solution.py:20
  31.9 2.9 %copy.662 = f32[16,8,1024]{2,1,0:T(8,128)S(1)} copy(f32[16,8,1024]{0,2,1:T(8,128)} %fusion.2) | data formatting | bytes 1048576 | tf_op jit(solution)/shard_map/add | solution.py:44
  37.2 3.0 %collective-permute-start.4 = (f32[4,1,1024]{2,0,1:T(4,128)S(1)}, f32[4,1,1024]{2,0,1:T(4,128)S(1)}, u32[]{:S(2)}, u32[]{:S(2)}) collective-permute-start(f32[4,1,1024]{2,0,1:T(4,128)S(1)} %get-tuple-element.174), channel_id=1, source_target_pairs={{0,2},{2,4},{4,6},{6,8},{8,10},{10,12},{12,14},{14,16},{16,18},{18... | collective-permute-start | bytes 49160 | tf_op jit(solution)/shard_map/ppermute | solution.py:20
  40.5 2.8 %gather_fusion.1 = f32[1024,4]{1,0:T(8,128)S(1)} fusion(f32[4,1024]{0,1:T(8,128)S(1)} %copy.673, s32[1024]{0:T(1024)S(1)} %fusion.62), kind=kCustom, calls=%fused_computation.1.clone | custom fusion | bytes 36864 | tf_op jit(solution)/shard_map/jit(_take)/gather | solution.py:72
  43.6 4.5 %collective-permute-start.6 = (f32[1,10,1024]{2,0,1:T(1,128)S(1)}, f32[1,10,1024]{2,0,1:T(1,128)S(1)}, u32[]{:S(2)}, u32[]{:S(2)}) collective-permute-start(f32[1,10,1024]{2,0,1:T(1,128)S(1)} %get-tuple-element.136), channel_id=1, source_target_pairs={{0,1},{2,3},{4,5},{6,7},{8,9},{10,11},{12,13},{14,15},{16,17},{18,... | collective-permute-start | bytes 122888 | tf_op jit(solution)/shard_map/ppermute | solution.py:20
  49.8 4.4 %collective-permute-done.7 = f32[1,10,1024]{2,0,1:T(1,128)S(1)} collective-permute-done((f32[1,10,1024]{2,0,1:T(1,128)S(1)}, f32[1,10,1024]{2,0,1:T(1,128)S(1)}, u32[]{:S(2)}, u32[]{:S(2)}) %collective-permute-start.7) | collective-permute-done | bytes 40992 | tf_op jit(solution)/shard_map/ppermute | solution.py:21
  56.3 3.0 %collective-permute-start.8 = (f32[4,1,1024]{2,0,1:T(4,128)S(1)}, f32[4,1,1024]{2,0,1:T(4,128)S(1)}, u32[]{:S(2)}, u32[]{:S(2)}) collective-permute-start(f32[4,1,1024]{2,0,1:T(4,128)S(1)} %get-tuple-element.167), channel_id=1, source_target_pairs={{0,2},{2,4},{4,6},{6,8},{8,10},{10,12},{12,14},{14,16},{16,18},{18... | collective-permute-start | bytes 49160 | tf_op jit(solution)/shard_map/ppermute | solution.py:20
  59.6 2.8 %gather_fusion.2 = f32[1024,4]{1,0:T(8,128)S(1)} fusion(f32[4,1024]{0,1:T(8,128)S(1)} %copy.680, s32[1024]{0:T(1024)S(1)} %fusion.62), kind=kCustom, calls=%fused_computation.2.clone | custom fusion | bytes 36864 | tf_op jit(solution)/shard_map/jit(_take)/gather | solution.py:72
  65.8 4.3 %collective-permute-done.11 = f32[1,10,1024]{2,0,1:T(1,128)S(1)} collective-permute-done((f32[1,10,1024]{2,0,1:T(1,128)S(1)}, f32[1,10,1024]{2,0,1:T(1,128)S(1)}, u32[]{:S(2)}, u32[]{:S(2)}) %collective-permute-start.11) | collective-permute-done | bytes 40992 | tf_op jit(solution)/shard_map/ppermute | solution.py:21
  73.4 3.0 %collective-permute-start.12 = (f32[4,1,1024]{2,0,1:T(4,128)S(1)}, f32[4,1,1024]{2,0,1:T(4,128)S(1)}, u32[]{:S(2)}, u32[]{:S(2)}) collective-permute-start(f32[4,1,1024]{2,0,1:T(4,128)S(1)} %get-tuple-element.160), channel_id=1, source_target_pairs={{0,2},{2,4},{4,6},{6,8},{8,10},{10,12},{12,14},{14,16},{16,18},{18... | collective-permute-start | bytes 49160 | tf_op jit(solution)/shard_map/ppermute | solution.py:20
  79.1 5.0 %fusion.1 = (f32[16,8,128]{0,2,1:T(8,128)S(1)}, f32[16,8,128]{0,2,1:T(8,128)S(1)}) fusion(f32[16,8,1024]{0,2,1:T(8,128)} %copy.687, f32[8]{0:T(128)S(1)} %get-tuple-element.188, f32[8]{0:T(128)S(1)} %get-tuple-element.189), kind=kLoop, calls=%fused_computation.9 | loop fusion | flops 491520 | bytes 655424 | tf_op jit(solution)/shard_map/reduce_sum | solution.py:53
  84.6 2.8 %gather_fusion.3 = f32[1024,4]{1,0:T(8,128)S(1)} fusion(f32[4,1024]{0,1:T(8,128)S(1)} %copy.695, s32[1024]{0:T(1024)S(1)} %fusion.62), kind=kCustom, calls=%fused_computation.3.clone | custom fusion | bytes 36864 | tf_op jit(solution)/shard_map/jit(_take)/gather | solution.py:72
  87.7 4.4 %all-gather = f32[32,2,128]{2,1,0:T(2,128)S(1)} all-gather(f32[16,2,128]{2,1,0:T(2,128)S(1)} %copy.688), channel_id=2, replica_groups=mesh['wide'=16,'lev'=2] {'lev'}, dimensions={0}, use_global_device_ids=true | all-gather | bytes 49152 | tf_op jit(solution)/shard_map/all_gather | solution.py:126
  92.7 6.9 %all-to-all-start.1 = ((f32[16,1,2,128]{3,2,1,0:T(2,128)}), f32[16,1,2,128]{3,2,1,0:T(2,128)S(1)}, u32[]{:S(2)}, u32[]{:S(2)}) async-start(f32[16,1,2,128]{3,2,1,0:T(2,128)} %copy.690), calls=%async_computation.1 | async-start | bytes 32768 | tf_op jit(solution)/shard_map/all_to_all | solution.py:128
  103.3 2.9 %all-to-all-done.1 = f32[16,1,2,128]{3,2,1,0:T(2,128)S(1)} async-done(((f32[16,1,2,128]{3,2,1,0:T(2,128)}), f32[16,1,2,128]{3,2,1,0:T(2,128)S(1)}, u32[]{:S(2)}, u32[]{:S(2)}) %all-to-all-start.1) | async-done | bytes 16416 | tf_op jit(solution)/shard_map/all_to_all | solution.py:128
  110.2 3.0 %collective-permute-start.16 = (f32[4,1,1024]{2,0,1:T(4,128)S(1)}, f32[4,1,1024]{2,0,1:T(4,128)S(1)}, u32[]{:S(2)}, u32[]{:S(2)}) collective-permute-start(f32[4,1,1024]{2,0,1:T(4,128)S(1)} %get-tuple-element.153), channel_id=1, source_target_pairs={{0,2},{2,4},{4,6},{6,8},{8,10},{10,12},{12,14},{14,16},{16,18},{18... | collective-permute-start | bytes 49160 | tf_op jit(solution)/shard_map/ppermute | solution.py:20
  113.5 2.8 %gather_fusion.4 = f32[1024,4]{1,0:T(8,128)S(1)} fusion(f32[4,1024]{0,1:T(8,128)S(1)} %copy.704, s32[1024]{0:T(1024)S(1)} %fusion.62), kind=kCustom, calls=%fused_computation.4.clone | custom fusion | bytes 36864 | tf_op jit(solution)/shard_map/jit(_take)/gather | solution.py:72
  120.6 4.5 %collective-permute-done.19 = f32[1,10,1024]{2,0,1:T(1,128)S(1)} collective-permute-done((f32[1,10,1024]{2,0,1:T(1,128)S(1)}, f32[1,10,1024]{2,0,1:T(1,128)S(1)}, u32[]{:S(2)}, u32[]{:S(2)}) %collective-permute-start.19) | collective-permute-done | bytes 40992 | tf_op jit(solution)/shard_map/ppermute | solution.py:21
  127.3 3.0 %collective-permute-start.20 = (f32[4,1,1024]{2,0,1:T(4,128)S(1)}, f32[4,1,1024]{2,0,1:T(4,128)S(1)}, u32[]{:S(2)}, u32[]{:S(2)}) collective-permute-start(f32[4,1,1024]{2,0,1:T(4,128)S(1)} %get-tuple-element.146), channel_id=1, source_target_pairs={{0,2},{2,4},{4,6},{6,8},{8,10},{10,12},{12,14},{14,16},{16,18},{18... | collective-permute-start | bytes 49160 | tf_op jit(solution)/shard_map/ppermute | solution.py:20
  130.6 2.8 %gather_fusion.5 = f32[1024,4]{1,0:T(8,128)S(1)} fusion(f32[4,1024]{0,1:T(8,128)S(1)} %copy.715, s32[1024]{0:T(1024)S(1)} %fusion.62), kind=kCustom, calls=%fused_computation.5.clone | custom fusion | bytes 36864 | tf_op jit(solution)/shard_map/jit(_take)/gather | solution.py:72
  137.1 4.5 %collective-permute-done.23 = f32[1,10,1024]{2,0,1:T(1,128)S(1)} collective-permute-done((f32[1,10,1024]{2,0,1:T(1,128)S(1)}, f32[1,10,1024]{2,0,1:T(1,128)S(1)}, u32[]{:S(2)}, u32[]{:S(2)}) %collective-permute-start.23) | collective-permute-done | bytes 40992 | tf_op jit(solution)/shard_map/ppermute | solution.py:21
  (181 shorter events, 50.3 us)
Async XLA Ops:
  2.7 20.8 %collective-permute-start.1 = (f32[4,1,1024]{2,0,1:T(4,128)S(1)}, f32[4,1,1024]{2,0,1:T(4,128)S(1)}, u32[]{:S(2)}, u32[]{:S(2)}) collective-permute-start(f32[4,1,1024]{2,0,1:T(4,128)S(1)} %get-tuple-element.180), channel_id=1, source_target_pairs={{2,0},{4,2},{6,4},{8,6},{10,8},{12,10},{14,12},{16,14},{18,16},{20... | collective-permute-start | bytes 49160 | tf_op jit(solution)/shard_map/ppermute | solution.py:21
  4.0 19.5 %collective-permute-start = (f32[4,1,1024]{2,0,1:T(4,128)S(1)}, f32[4,1,1024]{2,0,1:T(4,128)S(1)}, u32[]{:S(2)}, u32[]{:S(2)}) collective-permute-start(f32[4,1,1024]{2,0,1:T(4,128)S(1)} %get-tuple-element.181), channel_id=1, source_target_pairs={{0,2},{2,4},{4,6},{6,8},{8,10},{10,12},{12,14},{14,16},{16,18},{18... | collective-permute-start | bytes 49160 | tf_op jit(solution)/shard_map/ppermute | solution.py:20
  8.7 19.7 %all-to-all-start = ((f32[1,16,2,128]{3,2,0,1:T(2,128)}), f32[1,16,2,128]{3,2,0,1:T(2,128)S(1)}, u32[]{:S(2)}, u32[]{:S(2)}) async-start(f32[1,16,2,128]{3,2,0,1:T(2,128)} %copy.656), calls=%async_computation | async-start | bytes 32768 | tf_op jit(solution)/shard_map/all_to_all | solution.py:114
  23.6 11.4 %collective-permute-start.2 = (f32[1,10,1024]{2,0,1:T(1,128)S(1)}, f32[1,10,1024]{2,0,1:T(1,128)S(1)}, u32[]{:S(2)}, u32[]{:S(2)}) collective-permute-start(f32[1,10,1024]{2,0,1:T(1,128)S(1)} %get-tuple-element.138), channel_id=1, source_target_pairs={{0,1},{2,3},{4,5},{6,7},{8,9},{10,11},{12,13},{14,15},{16,17},{18,... | collective-permute-start | bytes 122888 | tf_op jit(solution)/shard_map/ppermute | solution.py:20
  27.1 8.0 %collective-permute-start.3 = (f32[1,10,1024]{2,0,1:T(1,128)S(1)}, f32[1,10,1024]{2,0,1:T(1,128)S(1)}, u32[]{:S(2)}, u32[]{:S(2)}) collective-permute-start(f32[1,10,1024]{2,0,1:T(1,128)S(1)} %get-tuple-element.139), channel_id=1, source_target_pairs={{1,0},{3,2},{5,4},{7,6},{9,8},{11,10},{13,12},{15,14},{17,16},{19,... | collective-permute-start | bytes 122888 | tf_op jit(solution)/shard_map/ppermute | solution.py:21
  35.9 7.7 %collective-permute-start.5 = (f32[4,1,1024]{2,0,1:T(4,128)S(1)}, f32[4,1,1024]{2,0,1:T(4,128)S(1)}, u32[]{:S(2)}, u32[]{:S(2)}) collective-permute-start(f32[4,1,1024]{2,0,1:T(4,128)S(1)} %get-tuple-element.173), channel_id=1, source_target_pairs={{2,0},{4,2},{6,4},{8,6},{10,8},{12,10},{14,12},{16,14},{18,16},{20... | collective-permute-start | bytes 49160 | tf_op jit(solution)/shard_map/ppermute | solution.py:21
  37.2 6.4 %collective-permute-start.4 = (f32[4,1,1024]{2,0,1:T(4,128)S(1)}, f32[4,1,1024]{2,0,1:T(4,128)S(1)}, u32[]{:S(2)}, u32[]{:S(2)}) collective-permute-start(f32[4,1,1024]{2,0,1:T(4,128)S(1)} %get-tuple-element.174), channel_id=1, source_target_pairs={{0,2},{2,4},{4,6},{6,8},{8,10},{10,12},{12,14},{14,16},{16,18},{18... | collective-permute-start | bytes 49160 | tf_op jit(solution)/shard_map/ppermute | solution.py:20
  43.6 6.2 %collective-permute-start.6 = (f32[1,10,1024]{2,0,1:T(1,128)S(1)}, f32[1,10,1024]{2,0,1:T(1,128)S(1)}, u32[]{:S(2)}, u32[]{:S(2)}) collective-permute-start(f32[1,10,1024]{2,0,1:T(1,128)S(1)} %get-tuple-element.136), channel_id=1, source_target_pairs={{0,1},{2,3},{4,5},{6,7},{8,9},{10,11},{12,13},{14,15},{16,17},{18,... | collective-permute-start | bytes 122888 | tf_op jit(solution)/shard_map/ppermute | solution.py:20
  48.2 6.0 %collective-permute-start.7 = (f32[1,10,1024]{2,0,1:T(1,128)S(1)}, f32[1,10,1024]{2,0,1:T(1,128)S(1)}, u32[]{:S(2)}, u32[]{:S(2)}) collective-permute-start(f32[1,10,1024]{2,0,1:T(1,128)S(1)} %get-tuple-element.137), channel_id=1, source_target_pairs={{1,0},{3,2},{5,4},{7,6},{9,8},{11,10},{13,12},{15,14},{17,16},{19,... | collective-permute-start | bytes 122888 | tf_op jit(solution)/shard_map/ppermute | solution.py:21
  55.0 7.7 %collective-permute-start.9 = (f32[4,1,1024]{2,0,1:T(4,128)S(1)}, f32[4,1,1024]{2,0,1:T(4,128)S(1)}, u32[]{:S(2)}, u32[]{:S(2)}) collective-permute-start(f32[4,1,1024]{2,0,1:T(4,128)S(1)} %get-tuple-element.166), channel_id=1, source_target_pairs={{2,0},{4,2},{6,4},{8,6},{10,8},{12,10},{14,12},{16,14},{18,16},{20... | collective-permute-start | bytes 49160 | tf_op jit(solution)/shard_map/ppermute | solution.py:21
  56.3 6.4 %collective-permute-start.8 = (f32[4,1,1024]{2,0,1:T(4,128)S(1)}, f32[4,1,1024]{2,0,1:T(4,128)S(1)}, u32[]{:S(2)}, u32[]{:S(2)}) collective-permute-start(f32[4,1,1024]{2,0,1:T(4,128)S(1)} %get-tuple-element.167), channel_id=1, source_target_pairs={{0,2},{2,4},{4,6},{6,8},{8,10},{10,12},{12,14},{14,16},{16,18},{18... | collective-permute-start | bytes 49160 | tf_op jit(solution)/shard_map/ppermute | solution.py:20
  64.2 5.9 %collective-permute-start.11 = (f32[1,10,1024]{2,0,1:T(1,128)S(1)}, f32[1,10,1024]{2,0,1:T(1,128)S(1)}, u32[]{:S(2)}, u32[]{:S(2)}) collective-permute-start(f32[1,10,1024]{2,0,1:T(1,128)S(1)} %get-tuple-element.135), channel_id=1, source_target_pairs={{1,0},{3,2},{5,4},{7,6},{9,8},{11,10},{13,12},{15,14},{17,16},{19,... | collective-permute-start | bytes 122888 | tf_op jit(solution)/shard_map/ppermute | solution.py:21
  72.1 27.6 %collective-permute-start.13 = (f32[4,1,1024]{2,0,1:T(4,128)S(1)}, f32[4,1,1024]{2,0,1:T(4,128)S(1)}, u32[]{:S(2)}, u32[]{:S(2)}) collective-permute-start(f32[4,1,1024]{2,0,1:T(4,128)S(1)} %get-tuple-element.159), channel_id=1, source_target_pairs={{2,0},{4,2},{6,4},{8,6},{10,8},{12,10},{14,12},{16,14},{18,16},{20... | collective-permute-start | bytes 49160 | tf_op jit(solution)/shard_map/ppermute | solution.py:21
  73.4 26.3 %collective-permute-start.12 = (f32[4,1,1024]{2,0,1:T(4,128)S(1)}, f32[4,1,1024]{2,0,1:T(4,128)S(1)}, u32[]{:S(2)}, u32[]{:S(2)}) collective-permute-start(f32[4,1,1024]{2,0,1:T(4,128)S(1)} %get-tuple-element.160), channel_id=1, source_target_pairs={{0,2},{2,4},{4,6},{6,8},{8,10},{10,12},{12,14},{14,16},{16,18},{18... | collective-permute-start | bytes 49160 | tf_op jit(solution)/shard_map/ppermute | solution.py:20
  92.7 13.4 %all-to-all-start.1 = ((f32[16,1,2,128]{3,2,1,0:T(2,128)}), f32[16,1,2,128]{3,2,1,0:T(2,128)S(1)}, u32[]{:S(2)}, u32[]{:S(2)}) async-start(f32[16,1,2,128]{3,2,1,0:T(2,128)} %copy.690), calls=%async_computation.1 | async-start | bytes 32768 | tf_op jit(solution)/shard_map/all_to_all | solution.py:128
  99.8 7.9 %collective-permute-start.14 = (f32[1,10,1024]{2,0,1:T(1,128)S(1)}, f32[1,10,1024]{2,0,1:T(1,128)S(1)}, u32[]{:S(2)}, u32[]{:S(2)}) collective-permute-start(f32[1,10,1024]{2,0,1:T(1,128)S(1)} %get-tuple-element.132), channel_id=1, source_target_pairs={{0,1},{2,3},{4,5},{6,7},{8,9},{10,11},{12,13},{14,15},{16,17},{18,... | collective-permute-start | bytes 122888 | tf_op jit(solution)/shard_map/ppermute | solution.py:20
  102.0 5.9 %collective-permute-start.15 = (f32[1,10,1024]{2,0,1:T(1,128)S(1)}, f32[1,10,1024]{2,0,1:T(1,128)S(1)}, u32[]{:S(2)}, u32[]{:S(2)}) collective-permute-start(f32[1,10,1024]{2,0,1:T(1,128)S(1)} %get-tuple-element.133), channel_id=1, source_target_pairs={{1,0},{3,2},{5,4},{7,6},{9,8},{11,10},{13,12},{15,14},{17,16},{19,... | collective-permute-start | bytes 122888 | tf_op jit(solution)/shard_map/ppermute | solution.py:21
  108.9 7.9 %collective-permute-start.17 = (f32[4,1,1024]{2,0,1:T(4,128)S(1)}, f32[4,1,1024]{2,0,1:T(4,128)S(1)}, u32[]{:S(2)}, u32[]{:S(2)}) collective-permute-start(f32[4,1,1024]{2,0,1:T(4,128)S(1)} %get-tuple-element.152), channel_id=1, source_target_pairs={{2,0},{4,2},{6,4},{8,6},{10,8},{12,10},{14,12},{16,14},{18,16},{20... | collective-permute-start | bytes 49160 | tf_op jit(solution)/shard_map/ppermute | solution.py:21
  110.2 6.6 %collective-permute-start.16 = (f32[4,1,1024]{2,0,1:T(4,128)S(1)}, f32[4,1,1024]{2,0,1:T(4,128)S(1)}, u32[]{:S(2)}, u32[]{:S(2)}) collective-permute-start(f32[4,1,1024]{2,0,1:T(4,128)S(1)} %get-tuple-element.153), channel_id=1, source_target_pairs={{0,2},{2,4},{4,6},{6,8},{8,10},{10,12},{12,14},{14,16},{16,18},{18... | collective-permute-start | bytes 49160 | tf_op jit(solution)/shard_map/ppermute | solution.py:20
  116.8 3.7 %collective-permute-start.18 = (f32[1,10,1024]{2,0,1:T(1,128)S(1)}, f32[1,10,1024]{2,0,1:T(1,128)S(1)}, u32[]{:S(2)}, u32[]{:S(2)}) collective-permute-start(f32[1,10,1024]{2,0,1:T(1,128)S(1)} %get-tuple-element.130), channel_id=1, source_target_pairs={{0,1},{2,3},{4,5},{6,7},{8,9},{10,11},{12,13},{14,15},{16,17},{18,... | collective-permute-start | bytes 122888 | tf_op jit(solution)/shard_map/ppermute | solution.py:20
  118.8 6.3 %collective-permute-start.19 = (f32[1,10,1024]{2,0,1:T(1,128)S(1)}, f32[1,10,1024]{2,0,1:T(1,128)S(1)}, u32[]{:S(2)}, u32[]{:S(2)}) collective-permute-start(f32[1,10,1024]{2,0,1:T(1,128)S(1)} %get-tuple-element.131), channel_id=1, source_target_pairs={{1,0},{3,2},{5,4},{7,6},{9,8},{11,10},{13,12},{15,14},{17,16},{19,... | collective-permute-start | bytes 122888 | tf_op jit(solution)/shard_map/ppermute | solution.py:21
  126.0 7.9 %collective-permute-start.21 = (f32[4,1,1024]{2,0,1:T(4,128)S(1)}, f32[4,1,1024]{2,0,1:T(4,128)S(1)}, u32[]{:S(2)}, u32[]{:S(2)}) collective-permute-start(f32[4,1,1024]{2,0,1:T(4,128)S(1)} %get-tuple-element.145), channel_id=1, source_target_pairs={{2,0},{4,2},{6,4},{8,6},{10,8},{12,10},{14,12},{16,14},{18,16},{20... | collective-permute-start | bytes 49160 | tf_op jit(solution)/shard_map/ppermute | solution.py:21
  127.3 6.6 %collective-permute-start.20 = (f32[4,1,1024]{2,0,1:T(4,128)S(1)}, f32[4,1,1024]{2,0,1:T(4,128)S(1)}, u32[]{:S(2)}, u32[]{:S(2)}) collective-permute-start(f32[4,1,1024]{2,0,1:T(4,128)S(1)} %get-tuple-element.146), channel_id=1, source_target_pairs={{0,2},{2,4},{4,6},{6,8},{8,10},{10,12},{12,14},{14,16},{16,18},{18... | collective-permute-start | bytes 49160 | tf_op jit(solution)/shard_map/ppermute | solution.py:20
  135.4 6.2 %collective-permute-start.23 = (f32[1,10,1024]{2,0,1:T(1,128)S(1)}, f32[1,10,1024]{2,0,1:T(1,128)S(1)}, u32[]{:S(2)}, u32[]{:S(2)}) collective-permute-start(f32[1,10,1024]{2,0,1:T(1,128)S(1)} %get-tuple-element.129), channel_id=1, source_target_pairs={{1,0},{3,2},{5,4},{7,6},{9,8},{11,10},{13,12},{15,14},{17,16},{19,... | collective-permute-start | bytes 122888 | tf_op jit(solution)/shard_map/ppermute | solution.py:21
  (9 other events, 153.5 us)
